TPU v7x, 32 devices: a whole 2x2x4 slice. The times are simulated.
32 devices in a mesh: fsdp: 4 (over z), ctx: 4 (over y, x), tp: 2 (over core).
Axes of the slice: x: 2, y: 2, z: 4, core: 2. Of those that a mesh axis runs over, the one named last changes fastest.
Arguments:
- block_input: bfloat16 [4, 1024, 1600], P('fsdp', 'ctx'), may hold values from -8 to 8
- segments: int32 [4, 1024], P('fsdp', 'ctx'), may hold values from 0 to 3, never falling along the last dimension, each value on 1 to 512 neighbouring positions
- ln1_gain: float32 [1600], replicated, may hold values from 0.5 to 1.5
- ln1_shift: float32 [1600], replicated, may hold values from -3 to 3
- qkv_weight: bfloat16 [1600, 4800], P('fsdp'), may hold values from -4 to 4
- out_weight: bfloat16 [1600, 1600], P(None, 'fsdp'), may hold values from -0.4375 to 0.4375
- ln2_gain: float32 [1600], replicated, may hold values from 0.5 to 1.5
- ln2_shift: float32 [1600], replicated, may hold values from -3 to 3
- fc_weight: bfloat16 [1600, 6400], P('fsdp', 'tp'), may hold values from -0.15625 to 0.15625
- proj_weight: bfloat16 [6400, 1600], P('tp', 'fsdp'), may hold values from -0.078125 to 0.078125
- cotangent: bfloat16 [4, 1024, 1600], P('fsdp', 'ctx'), may hold values from -6 to 6
Outputs:
- block_output: bfloat16 [4, 1024, 1600], P('fsdp', 'ctx')
- grad_input: float32 [4, 1024, 1600], P('fsdp', 'ctx')
- grad_ln1_gain: float32 [1600], P(('fsdp', 'ctx'))
- grad_ln1_shift: float32 [1600], P(('fsdp', 'ctx'))
- grad_qkv_weight: float32 [1600, 4800], P(('fsdp', 'ctx'))
- grad_out_weight: float32 [1600, 1600], P(None, ('fsdp', 'ctx'))
- grad_ln2_gain: float32 [1600], P(('fsdp', 'ctx'))
- grad_ln2_shift: float32 [1600], P(('fsdp', 'ctx'))
- grad_fc_weight: float32 [1600, 6400], P(('fsdp', 'ctx'), 'tp')
- grad_proj_weight: float32 [6400, 1600], P('tp', ('fsdp', 'ctx'))
All inputs are finite; a program needn't handle non-finite values.
Results may differ from a plain program's by a relative error of at most 0.013.
The roundings to bfloat16 on the way count: a program that leaves them out, or rounds other values in their place, can miss the bound.
Values may be sent and summed in bfloat16 or wider, within the bound.
A program may use at most 320 MiB of HBM per device.

v0:
```python
import jax
import jax.numpy as jnp
from jax import lax
from jax.sharding import PartitionSpec as P

H = 25
HD = 64
EPS = 1e-05
BF = jnp.bfloat16
F32 = jnp.float32
PLANE = ("ctx", "tp")


def dot(lhs, rhs, dims):
    return lax.dot_general(lhs, rhs, (dims, ((), ())), preferred_element_type=F32)


def moments(values):
    centered = values - jnp.mean(values, axis=-1, keepdims=True)
    inv_std = lax.rsqrt(jnp.mean(centered * centered, axis=-1, keepdims=True) + EPS)
    return (centered * inv_std, inv_std)


def norm_back(upstream, normed, inv_std, gain):
    scaled = upstream * gain
    return inv_std * (
        scaled
        - jnp.mean(scaled, axis=-1, keepdims=True)
        - normed * jnp.mean(scaled * normed, axis=-1, keepdims=True)
    )


def gelu_tanh(values):
    return jax.nn.gelu(values, approximate=True)


def masked_scores(queries, keys, seg):
    length = queries.shape[0]
    scores = jnp.einsum("qhd,khd->hqk", queries, keys, preferred_element_type=F32) * HD ** (-0.5)
    pos = jnp.arange(length, dtype=jnp.int32)
    allowed = (pos[None, :] <= pos[:, None]) & (seg[None, :] == seg[:, None])
    return jnp.where(allowed[None], scores, -1e30)


def attend(queries, keys, values, seg):
    scores = masked_scores(queries, keys, seg)
    row_max = jnp.max(scores, axis=-1, keepdims=True)
    exponent = jnp.exp(scores - row_max)
    total = jnp.sum(exponent, axis=-1, keepdims=True)
    probs = (exponent / total).astype(BF)
    attended = jnp.einsum("hqk,khd->qhd", probs, values, preferred_element_type=F32)
    return (attended.astype(BF), row_max + jnp.log(total))


def attend_back(queries, keys, values, seg, lse, grad):
    probs = jnp.exp(masked_scores(queries, keys, seg) - lse)
    grad_v = jnp.einsum("hqk,qhd->khd", probs.astype(BF), grad, preferred_element_type=F32)
    grad_p = jnp.einsum("qhd,khd->hqk", grad, values, preferred_element_type=F32)
    inner = jnp.sum(probs * grad_p, axis=-1, keepdims=True)
    raw = (probs * (grad_p - inner) * HD ** (-0.5)).astype(BF)
    grad_q = jnp.einsum("hqk,khd->qhd", raw, keys, preferred_element_type=F32)
    grad_k = jnp.einsum("hqk,qhd->khd", raw, queries, preferred_element_type=F32)
    return (grad_q, grad_k, grad_v)


def build(mesh):
    ctx_n, tp_n = (mesh.shape["ctx"], mesh.shape["tp"])
    members = ctx_n * tp_n
    slots = -(-H // members)
    starts = [m * H // members for m in range(members + 1)]
    counts = [starts[m + 1] - starts[m] for m in range(members)]
    width = slots * HD

    def local(x, segments, g1, b1, wqkv, wout, g2, b2, wfc, wproj, cot):
        x, cot = (x[0], cot[0])
        rows, model = x.shape
        tp_i, ctx_i = (lax.axis_index("tp"), lax.axis_index("ctx"))
        member = ctx_i * tp_n + tp_i
        own = rows // tp_n
        head0 = member * H // members
        head_n = (member + 1) * H // members - head0
        valid = jnp.arange(width, dtype=jnp.int32) < head_n * HD

        def cols(matrix, start, size):
            return lax.dynamic_slice_in_dim(matrix, start, size, 1)

        def rows_of(matrix, start, size):
            return lax.dynamic_slice_in_dim(matrix, start, size, 0)

        wq = jnp.concatenate([cols(wqkv, p * H * HD + head0 * HD, width) for p in range(3)], axis=1)
        wq = lax.all_gather(wq, "fsdp", axis=0, tiled=True)
        part = model // members
        wo = lax.all_gather(rows_of(wout, member * part, part), "fsdp", axis=1, tiled=True)
        wo = lax.all_gather(wo, PLANE, axis=0, tiled=True)
        hidden = wfc.shape[1] // ctx_n
        wf = lax.all_gather(cols(wfc, ctx_i * hidden, hidden), "fsdp", axis=0, tiled=True)
        wp = lax.all_gather(rows_of(wproj, ctx_i * hidden, hidden), "fsdp", axis=1, tiled=True)

        def to_plane(v):
            return lax.all_gather(v, PLANE, axis=0, tiled=True)

        def from_plane(v):
            return lax.psum_scatter(v, PLANE, scatter_dimension=0, tiled=True)

        x_own = rows_of(x, tp_i * own, own)
        cot_own = rows_of(cot, tp_i * own, own)
        x_all = to_plane(x_own)
        cot_all = to_plane(cot_own)
        seg = lax.all_gather(segments[0], "ctx", axis=0, tiled=True)
        length = x_all.shape[0]
        n1_all, _ = moments(x_all.astype(F32))
        h1 = (n1_all * g1 + b1).astype(BF)
        qkv = dot(h1, wq, ((1,), (0,))).astype(BF).reshape(length, 3, slots, HD)
        q, k, v = (qkv[:, 0], qkv[:, 1], qkv[:, 2])
        attended, lse = attend(q, k, v, seg)
        attended = attended.reshape(length, width)
        spread = lax.all_to_all(attended, PLANE, 0, 1, tiled=True)
        att_own = jnp.concatenate(
            [spread[:, m * width : m * width + counts[m] * HD] for m in range(members)], axis=1
        )
        x_own_f32 = x_own.astype(F32)
        r1 = x_own_f32 + dot(att_own, wo, ((1,), (0,)))
        n2, s2 = moments(r1)
        h2 = to_plane((n2 * g2 + b2).astype(BF))
        pre = dot(h2, wf, ((1,), (0,)))
        act, pull = jax.vjp(gelu_tanh, pre)
        act = act.astype(BF)
        mlp = from_plane(dot(act, wp, ((1,), (0,))))
        out = lax.all_gather((r1 + mlp).astype(BF), "tp", axis=0, tiled=True)
        grad_proj = dot(act, cot_all, ((0,), (0,)))
        grad_pre = pull(dot(cot_all, wp, ((1,), (1,))))[0].astype(BF)
        grad_fc = dot(h2, grad_pre, ((0,), (0,)))
        grad_h2 = from_plane(dot(grad_pre, wf, ((1,), (1,))))
        grad_r1 = cot_own.astype(F32) + norm_back(grad_h2, n2, s2, g2)
        grad_att = to_plane(grad_r1.astype(BF))
        wo_mine = rows_of(wo, head0 * HD, width)
        grad_out = dot(attended, grad_att, ((0,), (0,)))
        grad_attended = jnp.where(valid, dot(grad_att, wo_mine, ((1,), (1,))), 0.0).astype(BF)
        dq, dk, dv = attend_back(q, k, v, seg, lse, grad_attended.reshape(length, slots, HD))
        dqkv = jnp.stack([dq, dk, dv], axis=1).astype(BF).reshape(length, 3 * width)
        grad_qkv = dot(h1, dqkv, ((0,), (0,)))
        grad_h1 = from_plane(dot(dqkv, wq, ((1,), (1,))))
        n1, s1 = moments(x_own_f32)
        grad_x = grad_r1 + norm_back(grad_h1, n1, s1, g1)
        grad_x = lax.all_gather(grad_x, "tp", axis=0, tiled=True)

        def over_fsdp(v, dim):
            return lax.psum_scatter(v, "fsdp", scatter_dimension=dim, tiled=True)

        fc_out = lax.all_to_all(over_fsdp(grad_fc, 0), "ctx", 0, 1, tiled=True)
        proj_out = lax.all_to_all(over_fsdp(grad_proj, 1), "ctx", 1, 0, tiled=True)
        gq = over_fsdp(grad_qkv, 0).astype(BF)
        gq = gq.reshape(ctx_n, gq.shape[0] // ctx_n, 3 * width)
        gq = lax.all_gather(lax.all_to_all(gq, "ctx", 0, 0, tiled=True), "tp", axis=1)
        gq = gq.reshape((members,) + gq.shape[2:])
        qkv_out = jnp.concatenate(
            [
                gq[m][:, p * width : p * width + counts[m] * HD]
                for p in range(3)
                for m in range(members)
            ],
            axis=1,
        ).astype(F32)
        go = over_fsdp(grad_out, 1).astype(BF)
        go = lax.all_to_all(go, "ctx", 1, 0, tiled=True)
        go = lax.all_gather(go.reshape(ctx_n, width, go.shape[1]), "tp", axis=1)
        go = go.reshape((members,) + go.shape[2:])
        out_out = jnp.concatenate([go[m][: counts[m] * HD] for m in range(members)], axis=0)
        out_out = out_out.astype(F32)
        sums = jnp.stack(
            [
                jnp.sum(grad_h1 * n1, axis=0),
                jnp.sum(grad_h1, axis=0),
                jnp.sum(grad_h2 * n2, axis=0),
                jnp.sum(grad_h2, axis=0),
            ]
        )
        sums = lax.psum_scatter(
            lax.psum(sums, "tp"), ("fsdp", "ctx"), scatter_dimension=1, tiled=True
        )
        return (
            out[None],
            grad_x[None],
            sums[0],
            sums[1],
            qkv_out,
            out_out,
            sums[2],
            sums[3],
            fc_out,
            proj_out,
        )

    return local


def solution(mesh):
    placed = (
        P("fsdp", "ctx", None),
        P("fsdp", "ctx"),
        P(),
        P(),
        P("fsdp", None),
        P(None, "fsdp"),
        P(),
        P(),
        P("fsdp", "tp"),
        P("tp", "fsdp"),
        P("fsdp", "ctx", None),
    )
    both = ("fsdp", "ctx")
    return jax.shard_map(
        build(mesh),
        mesh=mesh,
        in_specs=placed,
        out_specs=(
            P("fsdp", "ctx", None),
            P("fsdp", "ctx", None),
            P(both),
            P(both),
            P(both, None),
            P(None, both),
            P(both),
            P(both),
            P(both, "tp"),
            P("tp", both),
        ),
        check_vma=False,
    )
```

profile of v0, /device:TPU:0, one launch (start us, length us, event | category | flops | bytes accessed | tf_op | source)
XLA Modules:
  0.0 1052.5 jit_solution(6024526135875657321)
XLA Ops:
  7.2 2.0 convert_reduce_fusion.1
  9.4 1.4 constant_dynamic-slice_fusion.6
  12.9 21.7 %all_gather.48 = bf16[200,1600]{0,1:T(8,128)(2,1)S(1)} all-gather(bf16[200,400]{0,1:T(8,128)(2,1)S(1)} %constant_dynamic-slice_fusion.3), channel_id=1, replica_groups=mesh['fsdp'=4,'ctx'=4,'tp'=2] {'fsdp'}, dimensions={1}, use_global_device_ids=true | all-gather | bytes 800000 | tf_op jit(solution)/shard_map/all_gather | solution.py:93
  35.8 1.2 constant_dynamic-slice_fusion.2
  37.0 8.2 all-gather.1
  46.5 2.7 convert_reduce_fusion
  50.4 50.2 %all-gather.16.cloned.1.call-done = bf16[1600,768]{1,0:T(8,128)(2,1)} async-done(((bf16[400,768]{1,0:T(8,128)(2,1)}), bf16[1600,768]{1,0:T(8,128)(2,1)}) %all-gather.16.cloned.1.call-update) | async-done | bytes 2457616 | tf_op jit(solution)/shard_map/all_gather | solution.py:91
  100.6 6.1 convolution_convert_fusion
  106.8 7.5 fusion.91
  114.3 8.0 fusion.4
  122.3 8.3 fusion.48
  130.7 17.1 %all_to_all.78 = bf16[8,128,256]{1,2,0:T(8,128)(2,1)S(1)} all-to-all(bf16[8,128,256]{1,2,0:T(8,128)(2,1)S(1)} %copy.96), channel_id=1, replica_groups=mesh['fsdp'=4,'ctx'=4,'tp'=2] {'ctx','tp'}, dimensions={0} | all-to-all | bytes 1048576 | tf_op jit(solution)/shard_map/all_to_all | solution.py:117
  148.0 4.7 fusion.92
  153.0 1.2 add_convert_fusion.1
  154.3 2.3 constant_dynamic-slice_fusion.1
  157.6 52.0 %all-gather.22.cloned.1.call-done = bf16[1600,800]{1,0:T(8,128)(2,1)} async-done(((bf16[400,800]{1,0:T(8,128)(2,1)}), bf16[1600,800]{1,0:T(8,128)(2,1)}) %all-gather.22.cloned.1.call-update) | async-done | bytes 2560016 | tf_op jit(solution)/shard_map/all_gather | solution.py:96
  209.6 34.3 %all-gather.20.cloned.1.call-done = bf16[1024,1600]{0,1:T(8,128)(2,1)} async-done(((bf16[128,1600]{0,1:T(8,128)(2,1)}), bf16[1024,1600]{0,1:T(8,128)(2,1)}) %all-gather.20.cloned.1.call-update) | async-done | bytes 3276816 | tf_op jit(solution)/shard_map/all_gather | solution.py:100
  243.9 7.6 fusion.93
  251.5 53.2 %all-gather.24.cloned.1.call-done = bf16[800,1600]{0,1:T(8,128)(2,1)} async-done(((bf16[800,400]{0,1:T(8,128)(2,1)}), bf16[800,1600]{0,1:T(8,128)(2,1)}) %all-gather.24.cloned.1.call-update) | async-done | bytes 2560016 | tf_op jit(solution)/shard_map/all_gather | solution.py:97
  304.8 34.5 %all-gather.32.cloned.1.call-done = bf16[1,1024,1600]{1,2,0:T(8,128)(2,1)} async-done(((bf16[1,128,1600]{1,2,0:T(8,128)(2,1)}), bf16[1,1024,1600]{1,2,0:T(8,128)(2,1)}) %all-gather.32.cloned.1.call-update) | async-done | bytes 3276816 | tf_op jit(solution)/shard_map/all_gather | solution.py:100
  339.2 9.0 fusion.31
  349.4 5.5 fusion.96
  354.9 63.0 %reduce-scatter.11.cloned.1.call-done = f32[128,1600]{0,1:T(8,128)} async-done(((f32[1024,1600]{0,1:T(8,128)}), f32[128,1600]{0,1:T(8,128)}) %reduce-scatter.11.cloned.1.call-update) | async-done | bytes 819216 | tf_op jit(solution)/shard_map/reduce_scatter | solution.py:103
  417.9 1.9 multiply_reduce_fusion.1
  419.8 2.2 fusion.77
  422.0 9.8 reduce-scatter.21.cloned.1.call-start
  431.8 9.1 fusion.32
  441.0 14.4 %all-gather.26.cloned.1.call-done = bf16[1024,1600]{0,1:T(8,128)(2,1)} async-done(((bf16[128,1600]{0,1:T(8,128)(2,1)}), bf16[1024,1600]{0,1:T(8,128)(2,1)}) %all-gather.26.cloned.1.call-update) | async-done | bytes 3276816 | tf_op jit(solution)/shard_map/all_gather | solution.py:100
  455.5 3.3 fusion.47
  458.8 10.0 fusion.71
  468.8 23.6 %fusion.55 = bf16[1024,1,4,64]{0,3,2,1:T(8,128)(2,1)} fusion(f32[4,1024,1024]{1,2,0:T(8,128)} %fusion.71, f32[4,1024,1024]{1,2,0:T(8,128)} %get-tuple-element.69, f32[4,1024]{1,0:T(4,128)S(1)} %log_add_fusion, bf16[1024,3,4,64]{0,3,2,1:T(8,128)(2,1)} %bitcast.215), kind=kOutput, calls=%fused_computation.52 | convolution fusion | flops 566498304 | bytes 68190208 | tf_op jit(solution)/shard_map/hqk,khd->qhd/dot_general | solution.py:61
  492.4 23.7 %fusion.52 = bf16[1024,1,4,64]{0,3,2,1:T(8,128)(2,1)} fusion(f32[4,1024,1024]{1,2,0:T(8,128)} %fusion.71, f32[4,1024,1024]{1,2,0:T(8,128)} %get-tuple-element.69, f32[4,1024]{1,0:T(4,128)S(1)} %log_add_fusion, bf16[1024,3,4,64]{0,3,2,1:T(8,128)(2,1)} %bitcast.216), kind=kOutput, calls=%fused_computation.51 | convolution fusion | flops 566498304 | bytes 68190208 | tf_op jit(solution)/shard_map/hqk,qhd->khd/dot_general | solution.py:62
  516.1 8.7 fusion.49
  526.2 4.6 fusion.97
  531.1 9.3 fusion.78
  540.4 8.4 fusion.95
  549.0 7.9 fusion.79
  556.9 4.1 fusion.94
  561.4 2.8 all_to_all.69
  564.1 4.3 all-to-all-start.4
  568.8 57.5 %reduce-scatter.13.cloned.1.call-done = f32[128,1600]{0,1:T(8,128)} async-done(((f32[1024,1600]{0,1:T(8,128)}), f32[128,1600]{0,1:T(8,128)}) %reduce-scatter.13.cloned.1.call-update) | async-done | bytes 819216 | tf_op jit(solution)/shard_map/reduce_scatter | solution.py:103
  626.3 1.9 fusion.69
  628.2 64.3 %reduce-scatter.9.cloned.1.call-done = f32[128,1600]{0,1:T(8,128)} async-done(((f32[1024,1600]{0,1:T(8,128)}), f32[128,1600]{0,1:T(8,128)}) %reduce-scatter.9.cloned.1.call-update) | async-done | bytes 819216 | tf_op jit(solution)/shard_map/reduce_scatter | solution.py:103
  692.5 2.9 fusion.68
  695.4 101.2 %reduce-scatter.19.cloned.1.call-done = f32[400,800]{1,0:T(8,128)} async-done(((f32[1600,800]{1,0:T(8,128)}), f32[400,800]{1,0:T(8,128)}) %reduce-scatter.19.cloned.1.call-update) | async-done | bytes 1280016 | tf_op jit(solution)/shard_map/reduce_scatter | solution.py:148
  796.6 2.6 all_to_all.65
  799.2 3.7 all-to-all-start.3
  802.9 84.9 %reduce-scatter.15.cloned.1.call-done = f32[400,768]{1,0:T(8,128)} async-done(((f32[1600,768]{1,0:T(8,128)}), f32[400,768]{1,0:T(8,128)}) %reduce-scatter.15.cloned.1.call-update) | async-done | bytes 1228816 | tf_op jit(solution)/shard_map/reduce_scatter | solution.py:148
  887.8 1.3 convert_element_type.82
  890.1 3.7 all-to-all-start.1
  893.8 33.8 %reduce-scatter.17.cloned.1.call-done = f32[256,400]{0,1:T(8,128)} async-done(((f32[256,1600]{0,1:T(8,128)}), f32[256,400]{0,1:T(8,128)}) %reduce-scatter.17.cloned.1.call-update) | async-done | bytes 409616 | tf_op jit(solution)/shard_map/reduce_scatter | solution.py:148
  929.3 3.7 all-to-all-start.2
  935.3 3.0 copy.119
  938.3 2.9 all_to_all.72
  941.2 1.5 copy.118
  942.6 2.9 all_to_all.68
  945.5 2.1 all-gather.4
  949.8 2.4 all_gather.53
  952.3 75.6 %all-reduce = f32[4,1600]{1,0:T(4,128)S(1)} all-reduce(f32[4,1600]{1,0:T(4,128)S(1)} %pad_maximum_fusion.2), channel_id=10, replica_groups=mesh['fsdp'=4,'ctx'=4,'tp'=2] {'fsdp','ctx'}, use_global_device_ids=true, to_apply=%region_21.22.clone | all-reduce | flops 6400 | bytes 51200
  1028.0 2.4 psum.8
  1031.0 1.4 copy.102
  1037.5 3.2 concatenate.14
  1040.7 2.8 convert_element_type.83
  1044.3 1.2 copy.161
  (151 shorter events, 24.1 us)
Async XLA Ops:
  7.2 28.6 %copy-start = (bf16[400,3200]{1,0:T(8,128)(2,1)S(1)}, bf16[400,3200]{1,0:T(8,128)(2,1)}, u32[]{:S(2)}) copy-start(bf16[400,3200]{1,0:T(8,128)(2,1)} %param.19) | copy-start | bytes 7680004
  7.2 39.3 %all-gather.30.cloned.1.call-start = ((), (), s32[]{:S(2)}) async-start(), calls=%async_computation.26 | async-start | bytes 3686400 | tf_op jit(solution)/shard_map/all_gather | solution.py:100
  9.3 91.3 %all-gather.16.cloned.1.call-start = ((), (), s32[]{:S(2)}) async-start(), calls=%async_computation.12 | async-start | bytes 3072000 | tf_op jit(solution)/shard_map/all_gather | solution.py:91
  11.7 25.3 %copy-start.15 = (s32[1,256]{1,0:T(1,128)S(1)}, s32[1,256]{1,0:T(1,128)}, u32[]{:S(2)}) copy-start(s32[1,256]{1,0:T(1,128)} %param.12) | copy-start | bytes 3076
  11.7 136.3 %all-gather.18.cloned.1.call-start = ((), (), s32[]{:S(2)}) async-start(), calls=%async_computation.13 | async-start | bytes 5990400 | tf_op jit(solution)/shard_map/all_gather | solution.py:94
  35.7 173.8 %all-gather.22.cloned.1.call-start = ((), (), s32[]{:S(2)}) async-start(), calls=%async_computation.15 | async-start | bytes 3584000 | tf_op jit(solution)/shard_map/all_gather | solution.py:96
  37.0 206.9 %all-gather.20.cloned.1.call-start = ((), (), s32[]{:S(2)}) async-start(), calls=%async_computation.14 | async-start | bytes 3686400 | tf_op jit(solution)/shard_map/all_gather | solution.py:100
  45.9 54.7 %copy-start.13 = (f32[1600]{0:T(1024)S(1)}, f32[1600]{0:T(1024)}, u32[]{:S(2)}) copy-start(f32[1600]{0:T(1024)} %param.13) | copy-start | bytes 19204
  46.5 2.9 copy-start.3
  46.5 54.1 %copy-start.18 = (f32[1600]{0:T(1024)S(1)}, f32[1600]{0:T(1024)}, u32[]{:S(2)}) copy-start(f32[1600]{0:T(1024)} %param.14) | copy-start | bytes 19204
  106.8 15.5 %copy-start.11 = (bf16[1024,768]{0,1:T(8,128)(2,1)}, bf16[1024,768]{0,1:T(8,128)(2,1)S(1)}, u32[]{:S(2)}) copy-start(bf16[1024,768]{0,1:T(8,128)(2,1)S(1)} %convolution_convert_fusion) | copy-start | bytes 4718596
  130.5 17.5 %copy-start.2 = (bf16[1,128,1600]{1,2,0:T(8,128)(2,1)S(1)}, bf16[1,128,1600]{1,2,0:T(8,128)(2,1)}, u32[]{:S(2)}) copy-start(bf16[1,128,1600]{1,2,0:T(8,128)(2,1)} %get-tuple-element.19) | copy-start | bytes 1228804
  148.0 5.0 copy-start.12
  148.0 5.0 copy-start.14
  152.7 4.0 copy-start.5
  154.2 150.5 %all-gather.24.cloned.1.call-start = ((), (), s32[]{:S(2)}) async-start(), calls=%async_computation.16 | async-start | bytes 3584000 | tf_op jit(solution)/shard_map/all_gather | solution.py:97
  156.6 182.6 %all-gather.32.cloned.1.call-start = ((), (), s32[]{:S(2)}) async-start(), calls=%async_computation.27 | async-start | bytes 3686400 | tf_op jit(solution)/shard_map/all_gather | solution.py:100
  157.5 260.3 %reduce-scatter.11.cloned.1.call-start = ((), (), s32[]{:S(2)}) async-start(), calls=%async_computation.18 | async-start | bytes 7372800 | tf_op jit(solution)/shard_map/reduce_scatter | solution.py:103
  339.2 10.2 copy-start.16
  348.2 1.2 copy-start.20
  354.9 100.6 %all-gather.26.cloned.1.call-start = ((), (), s32[]{:S(2)}) async-start(), calls=%async_computation.19 | async-start | bytes 3686400 | tf_op jit(solution)/shard_map/all_gather | solution.py:100
  422.0 139.3 %reduce-scatter.21.cloned.1.call-start = ((), (), s32[]{:S(2)}) async-start(), calls=%async_computation.25 | async-start | bytes 7168000 | tf_op jit(solution)/shard_map/reduce_scatter | solution.py:148
  440.9 185.4 %reduce-scatter.13.cloned.1.call-start = ((), (), s32[]{:S(2)}) async-start(), calls=%async_computation.20 | async-start | bytes 7372800 | tf_op jit(solution)/shard_map/reduce_scatter | solution.py:103
  516.1 8.7 copy-start.9
  516.1 8.7 copy-start.10
  516.1 10.1 copy-start.17
  525.0 1.1 copy-start.8
  530.8 161.7 %reduce-scatter.9.cloned.1.call-start = ((), (), s32[]{:S(2)}) async-start(), calls=%async_computation.17 | async-start | bytes 7372800 | tf_op jit(solution)/shard_map/reduce_scatter | solution.py:103
  540.4 256.2 %reduce-scatter.19.cloned.1.call-start = ((), (), s32[]{:S(2)}) async-start(), calls=%async_computation.24 | async-start | bytes 7168000 | tf_op jit(solution)/shard_map/reduce_scatter | solution.py:148
  548.9 338.9 %reduce-scatter.15.cloned.1.call-start = ((), (), s32[]{:S(2)}) async-start(), calls=%async_computation.22 | async-start | bytes 6144000 | tf_op jit(solution)/shard_map/reduce_scatter | solution.py:148
  556.8 370.7 %reduce-scatter.17.cloned.1.call-start = ((), (), s32[]{:S(2)}) async-start(), calls=%async_computation.23 | async-start | bytes 2048000 | tf_op jit(solution)/shard_map/reduce_scatter | solution.py:148
  561.3 131.2 %copy-start.4 = (f32[128,1600]{0,1:T(8,128)S(1)}, f32[128,1600]{0,1:T(8,128)}, u32[]{:S(2)}) copy-start(f32[128,1600]{0,1:T(8,128)} %reduce-scatter.11.cloned.1.call-done) | copy-start | bytes 2457604
  561.3 131.2 %copy-start.6 = (bf16[1,256,1600]{1,2,0:T(8,128)(2,1)S(1)}, bf16[1,256,1600]{1,2,0:T(8,128)(2,1)}, u32[]{:S(2)}) copy-start(bf16[1,256,1600]{1,2,0:T(8,128)(2,1)} %param.21) | copy-start | bytes 2457604
  564.1 235.1 %all-to-all-start.4 = ((f32[800,4,100]{0,2,1:T(8,128)}), f32[800,4,100]{0,2,1:T(8,128)}, u32[]{:S(2)}, u32[]{:S(2)}) async-start(f32[800,4,100]{0,2,1:T(8,128)} %all_to_all.69), calls=%async_computation.11 | async-start | bytes 2981888 | tf_op jit(solution)/shard_map/all_to_all | solution.py:151
  568.5 462.5 %all-gather.28.cloned.1.call-start = ((), (), s32[]{:S(2)}) async-start(), calls=%async_computation.21 | async-start | bytes 2457600 | tf_op jit(solution)/shard_map/all_gather | solution.py:145
  799.2 90.9 %all-to-all-start.3 = ((f32[4,100,800]{2,1,0:T(8,128)}), f32[4,100,800]{2,1,0:T(8,128)S(1)}, u32[]{:S(2)}, u32[]{:S(2)}) async-start(f32[4,100,800]{2,1,0:T(8,128)} %all_to_all.65), calls=%async_computation.9 | async-start | bytes 2981888 | tf_op jit(solution)/shard_map/all_to_all | solution.py:150
  889.2 44.9 %copy-start.19 = (u32[32]{0:T(128)S(1)}, u32[32]{0:T(128)}, u32[]{:S(2)}) copy-start(u32[32]{0:T(128)} %constant.100) | copy-start | bytes 388
  890.1 39.2 %all-to-all-start.1 = ((bf16[4,100,768]{2,1,0:T(8,128)(2,1)}), bf16[4,100,768]{2,1,0:T(8,128)(2,1)S(1)}, u32[]{:S(2)}, u32[]{:S(2)}) async-start(bf16[4,100,768]{2,1,0:T(8,128)(2,1)} %reshape.173), calls=%async_computation.5 | async-start | bytes 1277952 | tf_op jit(solution)/shard_map/all_to_all | solution.py:154
  929.3 16.2 %all-to-all-start.2 = ((bf16[256,4,100]{0,2,1:T(8,128)(2,1)}), bf16[256,4,100]{0,2,1:T(8,128)(2,1)S(1)}, u32[]{:S(2)}, u32[]{:S(2)}) async-start(bf16[256,4,100]{0,2,1:T(8,128)(2,1)} %all_to_all.62), calls=%async_computation.7 | async-start | bytes 425984 | tf_op jit(solution)/shard_map/all_to_all | solution.py:165
  933.0 98.0 %all-gather.34.cloned.1.call-start = ((), (), s32[]{:S(2)}) async-start(), calls=%async_computation.28 | async-start | bytes 1843200 | tf_op jit(solution)/shard_map/all_gather | solution.py:154
  1037.5 8.0 copy-start.1
  1040.7 3.7 copy-start.7
Sparse Core Ops, SparseCore 0:
  10.5 36.0 all-gather.29
  48.7 51.8 all-gather.15
  103.1 44.1 all-gather.17
  149.3 60.2 all-gather.21
  211.8 31.9 all-gather.19
  245.9 58.8 all-gather.23
  307.2 31.9 all-gather.31
  355.0 62.8 reduce-scatter.10
  422.1 33.2 all-gather.25
  457.7 101.7 reduce-scatter.20
  562.9 63.3 reduce-scatter.12
  629.6 62.8 reduce-scatter.8
  694.8 101.7 reduce-scatter.18
  798.8 88.9 reduce-scatter.14
  890.5 36.9 reduce-scatter.16
  929.5 8.4 all-gather.27
  939.9 10.4 all-gather.33
where the time goes:
time: 1060 us; the launch traced here: 1050 us
  waiting for transfers between devices  644 us (61%)
  matrix products  161 us (15%)
  blocking collectives  130 us (12%)
  local copies, waits for them, and re-layouts  43.3 us (4%)
  other arithmetic  32 us (3%)
  starting transfers between devices  26.2 us (2%)
  between operations  15.7 us (1%)
    reduce_scatter x4, waiting for transfers between devices, over_fsdp(): return lax.psum_scatter(v, 'fsdp', scatter_dimension=dim, tiled=True)  220 us
    reduce_scatter x3, waiting for transfers between devices, from_plane(): return lax.psum_scatter(v, PLANE, scatter_dimension=0, tiled=True)  185 us
    all_gather x4, waiting for transfers between devices, to_plane(): return lax.all_gather(v, PLANE, axis=0, tiled=True)  83.9 us
    dot_general x12, matrix products, dot(): lax.dot_general(lhs, rhs, (dims, ((), ())), preferred_element_type=F32)  79.7 us
    unnamed x1, blocking collectives  75.6 us
    all_gather x1, waiting for transfers between devices, local(): lax.all_gather(rows_of(wproj, ctx_i * hidden, hidden), 'fsdp', axis=1, ti...  53.2 us
    all_gather x1, waiting for transfers between devices, local(): lax.all_gather(cols(wfc, ctx_i * hidden, hidden), 'fsdp', axis=0, tiled=T...  52 us
    all_gather x1, waiting for transfers between devices, local(): wq = lax.all_gather(wq, 'fsdp', axis=0, tiled=True)  50.2 us
  transfers between devices with their start and end apart: 21, of which 13 were waited for; matrix products, arithmetic and copies ran while one was open for 18% of the time, Pallas kernels for 0%

commit v1 on v0

--- a/solution.py
+++ b/solution.py
@@ -9,6 +9,17 @@
 BF = jnp.bfloat16
 F32 = jnp.float32
 PLANE = ("ctx", "tp")
+
+
+def gather_around(array, axis, dim):
+    ways = lax.axis_size(axis)
+    pieces = [array]
+    for far in range(1, ways):
+        pieces.append(
+            lax.ppermute(pieces[far - 1], axis, [(d, (d - 1) % ways) for d in range(ways)])
+        )
+    line = jnp.concatenate(pieces, axis=dim)
+    return jnp.roll(line, lax.axis_index(axis) * array.shape[dim], axis=dim)
 
 
 def dot(lhs, rhs, dims):
@@ -88,7 +99,7 @@
             return lax.dynamic_slice_in_dim(matrix, start, size, 0)
 
         wq = jnp.concatenate([cols(wqkv, p * H * HD + head0 * HD, width) for p in range(3)], axis=1)
-        wq = lax.all_gather(wq, "fsdp", axis=0, tiled=True)
+        wq = gather_around(wq, "fsdp", 0)
         part = model // members
         wo = lax.all_gather(rows_of(wout, member * part, part), "fsdp", axis=1, tiled=True)
         wo = lax.all_gather(wo, PLANE, axis=0, tiled=True)

time: 1060 us -> 1010 us (0.953)
  waiting for transfers between devices: 644 us -> 578 us
    all_gather x1 -> x0, waiting for transfers between devices: 50.2 us -> none  [local(): wq = lax.all_gather(wq, 'fsdp', axis=0, tiled=True)]
    all_gather x1, waiting for transfers between devices: 52 us -> 6.34 us  [local(): lax.all_gather(cols(wfc, ctx_i * hidden, hidden), 'fsdp', axis=0, tiled=T...]
    ppermute x0 -> x3, waiting for transfers between devices: none -> 23.2 us  [gather_around(): lax.ppermute(pieces[far - 1], axis, [(d, (d - 1) % ways) for d in range(w...]
  transfers between devices with their start and end apart: 21 -> 23, of which waited for: 13 -> 13; matrix products, arithmetic and copies ran while one was open for 18% -> 20% of each run, Pallas kernels for 0% -> 0%
where the time goes in v1:
time: 1010 us; the launch traced here: 994 us
  waiting for transfers between devices  578 us (57%)
  matrix products  162 us (16%)
  blocking collectives  125 us (12%)
  local copies, waits for them, and re-layouts  53 us (5%)
  other arithmetic  33 us (3%)
  starting transfers between devices  27 us (3%)
  between operations  15.7 us (2%)
    reduce_scatter x4, waiting for transfers between devices, over_fsdp(): return lax.psum_scatter(v, 'fsdp', scatter_dimension=dim, tiled=True)  220 us
    reduce_scatter x3, waiting for transfers between devices, from_plane(): return lax.psum_scatter(v, PLANE, scatter_dimension=0, tiled=True)  183 us
    all_gather x4, waiting for transfers between devices, to_plane(): return lax.all_gather(v, PLANE, axis=0, tiled=True)  92.7 us
    dot_general x12, matrix products, dot(): lax.dot_general(lhs, rhs, (dims, ((), ())), preferred_element_type=F32)  80.9 us
    unnamed x1, blocking collectives  75.6 us
    all_gather x1, waiting for transfers between devices, local(): lax.all_gather(rows_of(wproj, ctx_i * hidden, hidden), 'fsdp', axis=1, ti...  53.2 us
    dot_general x1, matrix products, attend_back(): jnp.einsum('hqk,qhd->khd', raw, queries, preferred_element_type=F32)  23.7 us
    dot_general x1, matrix products, attend_back(): grad_q = jnp.einsum('hqk,khd->qhd', raw, keys, preferred_element_type=F32)  23.6 us
  transfers between devices with their start and end apart: 23, of which 13 were waited for; matrix products, arithmetic and copies ran while one was open for 20% of the time, Pallas kernels for 0%

profile of v1, /device:TPU:0, one launch (start us, length us, event | category | flops | bytes accessed | tf_op | source)
XLA Modules:
  0.0 994.3 jit_solution(4589829917894144289)
XLA Ops:
  7.2 2.0 convert_reduce_fusion.1
  10.5 21.7 %all_gather.44 = bf16[200,1600]{0,1:T(8,128)(2,1)S(1)} all-gather(bf16[200,400]{0,1:T(8,128)(2,1)S(1)} %constant_dynamic-slice_fusion.3), channel_id=1, replica_groups=mesh['fsdp'=4,'ctx'=4,'tp'=2] {'fsdp'}, dimensions={1}, use_global_device_ids=true | all-gather | bytes 800000 | tf_op jit(solution)/shard_map/all_gather | solution.py:104
  35.8 1.6 collective-permute-start
  37.5 12.0 %collective-permute-done = bf16[400,768]{1,0:T(8,128)(2,1)S(1)} collective-permute-done((bf16[400,768]{1,0:T(8,128)(2,1)S(1)}, bf16[400,768]{1,0:T(8,128)(2,1)S(1)}, u32[]{:S(2)}, u32[]{:S(2)}) %collective-permute-start) | collective-permute-done | bytes 614432 | tf_op jit(solution)/shard_map/ppermute | solution.py:19
  49.5 4.3 collective-permute-start.1
  53.8 11.2 %collective-permute-done.1 = bf16[400,768]{1,0:T(8,128)(2,1)} collective-permute-done((bf16[400,768]{1,0:T(8,128)(2,1)S(1)}, bf16[400,768]{1,0:T(8,128)(2,1)}, u32[]{:S(2)}, u32[]{:S(2)}) %collective-permute-start.1) | collective-permute-done | bytes 614432 | tf_op jit(solution)/shard_map/ppermute | solution.py:19
  64.9 4.4 collective-permute-start.2
  70.6 8.4 all-gather.1
  80.5 1.9 constant_dynamic-update-slice_fusion.5
  82.4 2.0 constant_dynamic-update-slice_fusion.4
  86.2 2.0 constant_dynamic-update-slice_fusion.1
  88.2 1.9 constant_dynamic-update-slice_fusion
  90.1 2.7 convert_reduce_fusion
  94.0 5.3 fusion.42
  99.3 7.4 fusion.100
  106.7 8.1 fusion.4
  114.8 7.5 fusion.55
  122.4 12.8 %all_to_all.78 = bf16[8,128,256]{1,2,0:T(8,128)(2,1)S(1)} all-to-all(bf16[8,128,256]{1,2,0:T(8,128)(2,1)S(1)} %copy.96), channel_id=1, replica_groups=mesh['fsdp'=4,'ctx'=4,'tp'=2] {'ctx','tp'}, dimensions={0} | all-to-all | bytes 1048576 | tf_op jit(solution)/shard_map/all_to_all | solution.py:128
  135.4 4.7 fusion.101
  141.7 2.3 constant_dynamic-slice_fusion.1
  145.0 6.3 all-gather.19.cloned.1.call-done
  151.3 34.3 %all-gather.17.cloned.1.call-done = bf16[1024,1600]{0,1:T(8,128)(2,1)} async-done(((bf16[128,1600]{0,1:T(8,128)(2,1)}), bf16[1024,1600]{0,1:T(8,128)(2,1)}) %all-gather.17.cloned.1.call-update) | async-done | bytes 3276816 | tf_op jit(solution)/shard_map/all_gather | solution.py:111
  185.7 7.7 fusion.102
  193.3 53.2 %all-gather.21.cloned.1.call-done = bf16[800,1600]{0,1:T(8,128)(2,1)} async-done(((bf16[800,400]{0,1:T(8,128)(2,1)}), bf16[800,1600]{0,1:T(8,128)(2,1)}) %all-gather.21.cloned.1.call-update) | async-done | bytes 2560016 | tf_op jit(solution)/shard_map/all_gather | solution.py:108
  246.5 34.3 %all-gather.29.cloned.1.call-done = bf16[1,1024,1600]{1,2,0:T(8,128)(2,1)} async-done(((bf16[1,128,1600]{1,2,0:T(8,128)(2,1)}), bf16[1,1024,1600]{1,2,0:T(8,128)(2,1)}) %all-gather.29.cloned.1.call-update) | async-done | bytes 3276816 | tf_op jit(solution)/shard_map/all_gather | solution.py:111
  280.9 9.0 fusion.31
  291.0 5.5 fusion.105
  296.6 63.0 %reduce-scatter.11.cloned.1.call-done = f32[128,1600]{0,1:T(8,128)} async-done(((f32[1024,1600]{0,1:T(8,128)}), f32[128,1600]{0,1:T(8,128)}) %reduce-scatter.11.cloned.1.call-update) | async-done | bytes 819216 | tf_op jit(solution)/shard_map/reduce_scatter | solution.py:114
  359.5 1.9 multiply_reduce_fusion.1
  361.4 2.2 fusion.86
  363.9 9.1 fusion.32
  373.1 24.0 %all-gather.23.cloned.1.call-done = bf16[1024,1600]{0,1:T(8,128)(2,1)} async-done(((bf16[128,1600]{0,1:T(8,128)(2,1)}), bf16[1024,1600]{0,1:T(8,128)(2,1)}) %all-gather.23.cloned.1.call-update) | async-done | bytes 3276816 | tf_op jit(solution)/shard_map/all_gather | solution.py:111
  397.1 3.3 fusion.54
  400.4 10.0 %fusion.78 = f32[4,1024,1024]{1,2,0:T(8,128)} fusion(bf16[1024,4,64]{0,2,1:T(8,128)(2,1)S(1)} %bitcast.192, bf16[1024,3,4,64]{0,3,2,1:T(8,128)(2,1)} %bitcast.212), kind=kOutput, calls=%fused_computation.85 | convolution fusion | flops 536870912 | bytes 17825792 | tf_op jit(solution)/shard_map/qhd,khd->hqk/dot_general | solution.py:69
  410.5 23.6 %fusion.62 = bf16[1024,1,4,64]{0,3,2,1:T(8,128)(2,1)} fusion(f32[4,1024,1024]{1,2,0:T(8,128)} %fusion.78, f32[4,1024,1024]{1,2,0:T(8,128)} %get-tuple-element.71, f32[4,1024]{1,0:T(4,128)S(1)} %log_add_fusion, bf16[1024,3,4,64]{0,3,2,1:T(8,128)(2,1)} %bitcast.213), kind=kOutput, calls=%fused_computation.56 | convolution fusion | flops 566498304 | bytes 68190208 | tf_op jit(solution)/shard_map/hqk,khd->qhd/dot_general | solution.py:72
  434.0 23.7 %fusion.59 = bf16[1024,1,4,64]{0,3,2,1:T(8,128)(2,1)} fusion(f32[4,1024,1024]{1,2,0:T(8,128)} %fusion.78, f32[4,1024,1024]{1,2,0:T(8,128)} %get-tuple-element.71, f32[4,1024]{1,0:T(4,128)S(1)} %log_add_fusion, bf16[1024,3,4,64]{0,3,2,1:T(8,128)(2,1)} %bitcast.214), kind=kOutput, calls=%fused_computation.55 | convolution fusion | flops 566498304 | bytes 68190208 | tf_op jit(solution)/shard_map/hqk,qhd->khd/dot_general | solution.py:73
  457.8 8.7 fusion.56
  467.8 6.4 fusion.38
  474.5 9.3 fusion.87
  483.8 8.5 fusion.104
  492.4 8.0 fusion.88
  500.4 4.2 fusion.103
  505.0 2.8 all_to_all.69
  507.8 4.4 all-to-all-start.4
  512.5 55.5 %reduce-scatter.13.cloned.1.call-done = f32[128,1600]{0,1:T(8,128)} async-done(((f32[1024,1600]{0,1:T(8,128)}), f32[128,1600]{0,1:T(8,128)}) %reduce-scatter.13.cloned.1.call-update) | async-done | bytes 819216 | tf_op jit(solution)/shard_map/reduce_scatter | solution.py:114
  568.0 1.9 fusion.76
  569.9 64.4 %reduce-scatter.9.cloned.1.call-done = f32[128,1600]{0,1:T(8,128)} async-done(((f32[1024,1600]{0,1:T(8,128)}), f32[128,1600]{0,1:T(8,128)}) %reduce-scatter.9.cloned.1.call-update) | async-done | bytes 819216 | tf_op jit(solution)/shard_map/reduce_scatter | solution.py:114
  634.3 2.9 fusion.75
  637.2 101.0 %reduce-scatter.19.cloned.1.call-done = f32[400,800]{1,0:T(8,128)} async-done(((f32[1600,800]{1,0:T(8,128)}), f32[400,800]{1,0:T(8,128)}) %reduce-scatter.19.cloned.1.call-update) | async-done | bytes 1280016 | tf_op jit(solution)/shard_map/reduce_scatter | solution.py:159
  738.3 2.6 all_to_all.65
  740.9 3.7 all-to-all-start.3
  744.6 85.1 %reduce-scatter.15.cloned.1.call-done = f32[400,768]{1,0:T(8,128)} async-done(((f32[1600,768]{1,0:T(8,128)}), f32[400,768]{1,0:T(8,128)}) %reduce-scatter.15.cloned.1.call-update) | async-done | bytes 1228816 | tf_op jit(solution)/shard_map/reduce_scatter | solution.py:159
  832.0 3.7 all-to-all-start.1
  835.6 33.8 %reduce-scatter.17.cloned.1.call-done = f32[256,400]{0,1:T(8,128)} async-done(((f32[256,1600]{0,1:T(8,128)}), f32[256,400]{0,1:T(8,128)}) %reduce-scatter.17.cloned.1.call-update) | async-done | bytes 409616 | tf_op jit(solution)/shard_map/reduce_scatter | solution.py:159
  871.1 3.7 all-to-all-start.2
  877.2 3.0 copy.119
  880.2 2.9 all_to_all.72
  884.5 2.9 all_to_all.68
  887.4 2.1 all-gather.4
  891.7 2.4 all_gather.49
  894.1 75.6 %all-reduce = f32[4,1600]{1,0:T(4,128)S(1)} all-reduce(f32[4,1600]{1,0:T(4,128)S(1)} %pad_maximum_fusion.2), channel_id=10, replica_groups=mesh['fsdp'=4,'ctx'=4,'tp'=2] {'fsdp','ctx'}, use_global_device_ids=true, to_apply=%region_21.22.clone | all-reduce | flops 6400 | bytes 51200
  969.8 2.4 psum.8
  979.3 3.2 concatenate.21
  982.5 2.8 convert_element_type.83
  (167 shorter events, 35.6 us)
Async XLA Ops:
  7.2 62.2 %copy-start = (bf16[400,3200]{1,0:T(8,128)(2,1)S(1)}, bf16[400,3200]{1,0:T(8,128)(2,1)}, u32[]{:S(2)}) copy-start(bf16[400,3200]{1,0:T(8,128)(2,1)} %param.19) | copy-start | bytes 7680004
  7.2 82.9 %all-gather.27.cloned.1.call-start = ((), (), s32[]{:S(2)}) async-start(), calls=%async_computation.25 | async-start | bytes 3686400 | tf_op jit(solution)/shard_map/all_gather | solution.py:111
  9.3 126.1 %all-gather.15.cloned.1.call-start = ((), (), s32[]{:S(2)}) async-start(), calls=%async_computation.12 | async-start | bytes 5990400 | tf_op jit(solution)/shard_map/all_gather | solution.py:105
  33.3 37.3 %copy-start.19 = (s32[1,256]{1,0:T(1,128)S(1)}, s32[1,256]{1,0:T(1,128)}, u32[]{:S(2)}) copy-start(s32[1,256]{1,0:T(1,128)} %param.12) | copy-start | bytes 3076
  33.3 118.0 %all-gather.19.cloned.1.call-start = ((), (), s32[]{:S(2)}) async-start(), calls=%async_computation.14 | async-start | bytes 3584000 | tf_op jit(solution)/shard_map/all_gather | solution.py:107
  34.9 14.6 %copy-start.7 = (bf16[400,256]{1,0:T(8,128)(2,1)}, bf16[400,256]{1,0:T(8,128)(2,1)S(1)}, u32[]{:S(2)}) copy-start(bf16[400,256]{1,0:T(8,128)(2,1)S(1)} %get-tuple-element.21) | copy-start | bytes 614404
  34.9 14.6 %copy-start.9 = (bf16[400,256]{1,0:T(8,128)(2,1)}, bf16[400,256]{1,0:T(8,128)(2,1)S(1)}, u32[]{:S(2)}) copy-start(bf16[400,256]{1,0:T(8,128)(2,1)S(1)} %get-tuple-element.22) | copy-start | bytes 614404
  35.8 13.7 %collective-permute-start = (bf16[400,768]{1,0:T(8,128)(2,1)S(1)}, bf16[400,768]{1,0:T(8,128)(2,1)S(1)}, u32[]{:S(2)}, u32[]{:S(2)}) collective-permute-start(bf16[400,768]{1,0:T(8,128)(2,1)S(1)} %get-tuple-element.33), channel_id=1, source_target_pairs={{0,24},{8,0},{16,8},{24,16},{1,25},{9,1},{17,9},{25,17},{2,26},{10... | collective-permute-start | bytes 1843208 | tf_op jit(solution)/shard_map/ppermute | solution.py:19
  49.5 15.4 %collective-permute-start.1 = (bf16[400,768]{1,0:T(8,128)(2,1)S(1)}, bf16[400,768]{1,0:T(8,128)(2,1)}, u32[]{:S(2)}, u32[]{:S(2)}) collective-permute-start(bf16[400,768]{1,0:T(8,128)(2,1)S(1)} %collective-permute-done), channel_id=1, source_target_pairs={{0,24},{8,0},{16,8},{24,16},{1,25},{9,1},{17,9},{25,17},{2,26},{10... | collective-permute-start | bytes 1843208 | tf_op jit(solution)/shard_map/ppermute | solution.py:19
  64.9 17.5 %collective-permute-start.2 = (bf16[400,768]{1,0:T(8,128)(2,1)}, bf16[400,768]{1,0:T(8,128)(2,1)}, u32[]{:S(2)}, u32[]{:S(2)}) collective-permute-start(bf16[400,768]{1,0:T(8,128)(2,1)} %collective-permute-done.1), channel_id=1, source_target_pairs={{0,24},{8,0},{16,8},{24,16},{1,25},{9,1},{17,9},{25,17},{2,26},{10... | collective-permute-start | bytes 1843208 | tf_op jit(solution)/shard_map/ppermute | solution.py:19
  70.5 13.9 %copy-start.8 = (bf16[400,256]{1,0:T(8,128)(2,1)S(1)}, bf16[400,256]{1,0:T(8,128)(2,1)}, u32[]{:S(2)}) copy-start(bf16[400,256]{1,0:T(8,128)(2,1)} %copy-done.7) | copy-start | bytes 614404
  70.5 13.9 %copy-start.10 = (bf16[400,256]{1,0:T(8,128)(2,1)S(1)}, bf16[400,256]{1,0:T(8,128)(2,1)}, u32[]{:S(2)}) copy-start(bf16[400,256]{1,0:T(8,128)(2,1)} %copy-done.9) | copy-start | bytes 614404
  70.5 115.1 %all-gather.17.cloned.1.call-start = ((), (), s32[]{:S(2)}) async-start(), calls=%async_computation.13 | async-start | bytes 3686400 | tf_op jit(solution)/shard_map/all_gather | solution.py:111
  90.1 3.8 copy-start.17
  90.1 2.9 copy-start.3
  90.1 3.9 copy-start.21
  99.3 15.5 %copy-start.15 = (bf16[1024,768]{0,1:T(8,128)(2,1)}, bf16[1024,768]{0,1:T(8,128)(2,1)S(1)}, u32[]{:S(2)}) copy-start(bf16[1024,768]{0,1:T(8,128)(2,1)S(1)} %fusion.42) | copy-start | bytes 4718596
  122.2 13.2 %copy-start.2 = (bf16[1,128,1600]{1,2,0:T(8,128)(2,1)S(1)}, bf16[1,128,1600]{1,2,0:T(8,128)(2,1)}, u32[]{:S(2)}) copy-start(bf16[1,128,1600]{1,2,0:T(8,128)(2,1)} %get-tuple-element.19) | copy-start | bytes 1228804
  135.4 5.0 copy-start.16
  135.4 5.0 copy-start.18
  140.1 4.0 copy-start.5
  141.7 104.8 %all-gather.21.cloned.1.call-start = ((), (), s32[]{:S(2)}) async-start(), calls=%async_computation.15 | async-start | bytes 3584000 | tf_op jit(solution)/shard_map/all_gather | solution.py:108
  144.1 136.8 %all-gather.29.cloned.1.call-start = ((), (), s32[]{:S(2)}) async-start(), calls=%async_computation.26 | async-start | bytes 3686400 | tf_op jit(solution)/shard_map/all_gather | solution.py:111
  145.0 214.5 %reduce-scatter.11.cloned.1.call-start = ((), (), s32[]{:S(2)}) async-start(), calls=%async_computation.17 | async-start | bytes 7372800 | tf_op jit(solution)/shard_map/reduce_scatter | solution.py:114
  280.9 10.2 %copy-start.20 = (bf16[1600,800]{1,0:T(8,128)(2,1)S(1)}, bf16[1600,800]{1,0:T(8,128)(2,1)}, u32[]{:S(2)}) copy-start(bf16[1600,800]{1,0:T(8,128)(2,1)} %all-gather.19.cloned.1.call-done) | copy-start | bytes 7680004
  289.9 1.2 copy-start.23
  296.5 100.6 %all-gather.23.cloned.1.call-start = ((), (), s32[]{:S(2)}) async-start(), calls=%async_computation.18 | async-start | bytes 3686400 | tf_op jit(solution)/shard_map/all_gather | solution.py:111
  363.7 141.3 %reduce-scatter.21.cloned.1.call-start = ((), (), s32[]{:S(2)}) async-start(), calls=%async_computation.24 | async-start | bytes 7168000 | tf_op jit(solution)/shard_map/reduce_scatter | solution.py:159
  373.0 195.0 %reduce-scatter.13.cloned.1.call-start = ((), (), s32[]{:S(2)}) async-start(), calls=%async_computation.19 | async-start | bytes 7372800 | tf_op jit(solution)/shard_map/reduce_scatter | solution.py:114
  457.8 8.7 copy-start.13
  457.8 8.7 copy-start.14
  466.6 1.1 copy-start.12
  474.2 160.1 %reduce-scatter.9.cloned.1.call-start = ((), (), s32[]{:S(2)}) async-start(), calls=%async_computation.16 | async-start | bytes 7372800 | tf_op jit(solution)/shard_map/reduce_scatter | solution.py:114
  483.8 254.5 %reduce-scatter.19.cloned.1.call-start = ((), (), s32[]{:S(2)}) async-start(), calls=%async_computation.23 | async-start | bytes 7168000 | tf_op jit(solution)/shard_map/reduce_scatter | solution.py:159
  492.3 337.3 %reduce-scatter.15.cloned.1.call-start = ((), (), s32[]{:S(2)}) async-start(), calls=%async_computation.21 | async-start | bytes 6144000 | tf_op jit(solution)/shard_map/reduce_scatter | solution.py:159
  500.4 369.0 %reduce-scatter.17.cloned.1.call-start = ((), (), s32[]{:S(2)}) async-start(), calls=%async_computation.22 | async-start | bytes 2048000 | tf_op jit(solution)/shard_map/reduce_scatter | solution.py:159
  504.9 129.4 %copy-start.4 = (f32[128,1600]{0,1:T(8,128)S(1)}, f32[128,1600]{0,1:T(8,128)}, u32[]{:S(2)}) copy-start(f32[128,1600]{0,1:T(8,128)} %reduce-scatter.11.cloned.1.call-done) | copy-start | bytes 2457604
  504.9 129.4 %copy-start.6 = (bf16[1,256,1600]{1,2,0:T(8,128)(2,1)S(1)}, bf16[1,256,1600]{1,2,0:T(8,128)(2,1)}, u32[]{:S(2)}) copy-start(bf16[1,256,1600]{1,2,0:T(8,128)(2,1)} %param.21) | copy-start | bytes 2457604
  507.8 233.2 %all-to-all-start.4 = ((f32[800,4,100]{0,2,1:T(8,128)}), f32[800,4,100]{0,2,1:T(8,128)}, u32[]{:S(2)}, u32[]{:S(2)}) async-start(f32[800,4,100]{0,2,1:T(8,128)} %all_to_all.69), calls=%async_computation.11 | async-start | bytes 2981888 | tf_op jit(solution)/shard_map/all_to_all | solution.py:162
  512.2 460.6 %all-gather.25.cloned.1.call-start = ((), (), s32[]{:S(2)}) async-start(), calls=%async_computation.20 | async-start | bytes 2457600 | tf_op jit(solution)/shard_map/all_gather | solution.py:156
  740.9 91.0 %all-to-all-start.3 = ((f32[4,100,800]{2,1,0:T(8,128)}), f32[4,100,800]{2,1,0:T(8,128)S(1)}, u32[]{:S(2)}, u32[]{:S(2)}) async-start(f32[4,100,800]{2,1,0:T(8,128)} %all_to_all.65), calls=%async_computation.9 | async-start | bytes 2981888 | tf_op jit(solution)/shard_map/all_to_all | solution.py:161
  831.0 44.9 %copy-start.22 = (u32[32]{0:T(128)S(1)}, u32[32]{0:T(128)}, u32[]{:S(2)}) copy-start(u32[32]{0:T(128)} %constant.121) | copy-start | bytes 388
  832.0 39.2 %all-to-all-start.1 = ((bf16[4,100,768]{2,1,0:T(8,128)(2,1)}), bf16[4,100,768]{2,1,0:T(8,128)(2,1)S(1)}, u32[]{:S(2)}, u32[]{:S(2)}) async-start(bf16[4,100,768]{2,1,0:T(8,128)(2,1)} %reshape.173), calls=%async_computation.5 | async-start | bytes 1277952 | tf_op jit(solution)/shard_map/all_to_all | solution.py:165
  871.1 16.2 %all-to-all-start.2 = ((bf16[256,4,100]{0,2,1:T(8,128)(2,1)}), bf16[256,4,100]{0,2,1:T(8,128)(2,1)S(1)}, u32[]{:S(2)}, u32[]{:S(2)}) async-start(bf16[256,4,100]{0,2,1:T(8,128)(2,1)} %all_to_all.62), calls=%async_computation.7 | async-start | bytes 425984 | tf_op jit(solution)/shard_map/all_to_all | solution.py:176
  874.8 98.0 %all-gather.31.cloned.1.call-start = ((), (), s32[]{:S(2)}) async-start(), calls=%async_computation.27 | async-start | bytes 1843200 | tf_op jit(solution)/shard_map/all_gather | solution.py:165
  979.3 8.0 copy-start.1
  982.5 3.7 copy-start.11
Sparse Core Ops, SparseCore 0:
  10.5 36.0 all-gather.26
  49.0 41.3 all-gather.14
  92.5 58.8 all-gather.18
  153.6 31.9 all-gather.16
  187.7 58.8 all-gather.20
  248.8 31.9 all-gather.28
  296.6 62.8 reduce-scatter.10
  363.8 33.2 all-gather.22
  399.5 101.7 reduce-scatter.20
  504.5 63.4 reduce-scatter.12
  571.5 62.8 reduce-scatter.8
  636.5 101.7 reduce-scatter.18
  740.6 88.9 reduce-scatter.14
  832.4 36.9 reduce-scatter.16
  871.4 8.4 all-gather.24
  881.8 10.4 all-gather.30
